TPU v7x, 32 devices: a whole 2x2x4 slice. The times are simulated.
32 devices in a mesh: tm: 4 (over y, x), space: 8 (over z, core).
Axes of the slice: x: 2, y: 2, z: 4, core: 2. Of those that a mesh axis runs over, the one named last changes fastest.
Arguments:
- queries: bfloat16 [4096, 4096], P(('tm', 'space')), may hold values from -20 to 20
- key_vectors: bfloat16 [4096, 4096], P(('tm', 'space')), may hold values from -20 to 20
- value_vectors: bfloat16 [4096, 4096], P(('tm', 'space')), may hold values from -6 to 6
- out_weight: bfloat16 [4096, 6144], P(None, 'space'), may hold values from -0.375 to 0.375
- frame_mask: int32 [4, 4], replicated, may hold values 0 or 1
Outputs:
- projected: bfloat16 [4096, 6144], P('tm', 'space')
All inputs are finite; a program needn't handle non-finite values.
Results may differ from a plain program's by a relative error of at most 0.0075.
Values may be sent and summed in bfloat16 or wider, within the bound.
A program may use at most 128 MiB of HBM per device.

v0:
```python
import math

import jax
import jax.numpy as jnp
from jax import lax
from jax.sharding import PartitionSpec as P

HD = 128


def passed_along(x, axis, by):
    devices = lax.axis_size(axis)
    return lax.ppermute(x, axis, [(i, (i + by) % devices) for i in range(devices)])


def block_update(state, query_blocks, arrived, allowed, scale_factor):
    run_max, run_total, run_sum = state
    keys_here = arrived[0]
    values_here = arrived[1]

    def one_block(pieces):
        query_part, old_max, old_total, old_sum = pieces
        scores = (
            jnp.einsum("qhd,khd->qhk", query_part, keys_here, preferred_element_type=jnp.float32)
            * scale_factor
        )
        block_max = jnp.where(allowed, jnp.max(scores, axis=2), -jnp.inf)
        new_max = jnp.maximum(old_max, block_max)
        exp_terms = jnp.where(allowed, jnp.exp(scores - new_max[:, :, None]), 0.0)
        rescale = jnp.exp(old_max - new_max)
        new_total = old_total * rescale + jnp.sum(exp_terms, axis=2)
        new_sum = old_sum * rescale[:, :, None] + jnp.einsum(
            "qhk,khd->qhd",
            exp_terms.astype(jnp.bfloat16),
            values_here,
            preferred_element_type=jnp.float32,
        )
        return (new_max, new_total, new_sum)

    return lax.map(one_block, (query_blocks, run_max, run_total, run_sum))


def mask_bit(frame_mask, row_index, column_index):
    count = frame_mask.shape[0]
    grid_rows = lax.broadcasted_iota(jnp.int32, (count, count), 0)
    grid_cols = lax.broadcasted_iota(jnp.int32, (count, count), 1)
    return jnp.sum(jnp.where((grid_rows == row_index) & (grid_cols == column_index), frame_mask, 0))


def body(queries, key_vectors, value_vectors, out_weight, frame_mask):
    frames = lax.axis_size("tm")
    here = lax.axis_index("tm")
    head_queries, head_keys, head_values = (
        lax.all_to_all(queries, "space", split_axis=1, concat_axis=0, tiled=True),
        lax.all_to_all(key_vectors, "space", split_axis=1, concat_axis=0, tiled=True),
        lax.all_to_all(value_vectors, "space", split_axis=1, concat_axis=0, tiled=True),
    )
    row_count = head_queries.shape[0]
    local_heads = head_queries.shape[1] // HD
    scale_factor = 1.0 / math.sqrt(HD)
    block_rows = 512
    block_count = row_count // block_rows
    query_blocks = head_queries.reshape(block_count, block_rows, local_heads, HD)
    pair = jnp.stack([head_keys, head_values]).reshape(2, row_count, local_heads, HD)
    state = (
        jnp.full((block_count, block_rows, local_heads), -jnp.inf, jnp.float32),
        jnp.zeros((block_count, block_rows, local_heads), jnp.float32),
        jnp.zeros((block_count, block_rows, local_heads, HD), jnp.float32),
    )
    state = block_update(state, query_blocks, pair, True, scale_factor)

    def visit(current, arrived, source):
        source_block = jnp.mod(source, frames)
        granted = mask_bit(frame_mask, here, source_block) == 1
        return block_update(current, query_blocks, arrived, granted, scale_factor)

    lower = pair
    upper = pair
    lower = passed_along(lower, "tm", 1)
    upper = passed_along(upper, "tm", -1)
    state = visit(state, lower, here - 1)
    state = visit(state, upper, here + 1)
    run_max, run_total, run_sum = state
    attended = (
        (run_sum / run_total[:, :, :, None])
        .reshape(row_count, local_heads * HD)
        .astype(jnp.bfloat16)
    )
    projected = jnp.dot(
        lax.all_gather(attended, "space", axis=1, tiled=True),
        out_weight,
        preferred_element_type=jnp.float32,
    )
    return projected.astype(jnp.bfloat16)


def solution(mesh):
    in_specs = (
        P(("tm", "space"), None),
        P(("tm", "space"), None),
        P(("tm", "space"), None),
        P(None, "space"),
        P(),
    )
    out_specs = P("tm", "space")
    return jax.shard_map(body, mesh=mesh, in_specs=in_specs, out_specs=out_specs, check_vma=False)
```

profile of v0, /device:TPU:0, one launch (start us, length us, event | category | flops | bytes accessed | tf_op | source)
XLA Modules:
  0.0 311.0 jit_solution(401340638023929092)
XLA Ops:
  6.5 2.3 copy.20
  8.9 6.4 %all-to-all-start.1 = ((bf16[128,8,512]{0,2,1:T(8,128)(2,1)}), bf16[128,8,512]{0,2,1:T(8,128)(2,1)S(1)}, u32[]{:S(2)}, u32[]{:S(2)}) async-start(bf16[128,8,512]{0,2,1:T(8,128)(2,1)} %bitcast.23), calls=%async_computation.1 | async-start | bytes 2097152 | tf_op jit(solution)/shard_map/all_to_all | solution.py:55
  15.2 2.3 copy.22
  17.5 24.3 %all-to-all-done.1 = bf16[128,8,512]{0,2,1:T(8,128)(2,1)S(1)} async-done(((bf16[128,8,512]{0,2,1:T(8,128)(2,1)}), bf16[128,8,512]{0,2,1:T(8,128)(2,1)S(1)}, u32[]{:S(2)}, u32[]{:S(2)}) %all-to-all-start.1) | async-done | bytes 1048608 | tf_op jit(solution)/shard_map/all_to_all | solution.py:55
  41.8 3.6 %all-to-all-start.2 = ((bf16[128,8,512]{0,2,1:T(8,128)(2,1)}), bf16[128,8,512]{0,2,1:T(8,128)(2,1)S(1)}, u32[]{:S(2)}, u32[]{:S(2)}) async-start(bf16[128,8,512]{0,2,1:T(8,128)(2,1)} %bitcast.25), calls=%async_computation.2 | async-start | bytes 2097152 | tf_op jit(solution)/shard_map/all_to_all | solution.py:56
  46.4 25.4 %all-to-all-done.2 = bf16[128,8,512]{0,2,1:T(8,128)(2,1)S(1)} async-done(((bf16[128,8,512]{0,2,1:T(8,128)(2,1)}), bf16[128,8,512]{0,2,1:T(8,128)(2,1)S(1)}, u32[]{:S(2)}, u32[]{:S(2)}) %all-to-all-start.2) | async-done | bytes 1048608 | tf_op jit(solution)/shard_map/all_to_all | solution.py:56
  72.8 3.6 %all-to-all-start = ((bf16[128,8,512]{2,0,1:T(8,128)(2,1)}), bf16[128,8,512]{2,0,1:T(8,128)(2,1)S(1)}, u32[]{:S(2)}, u32[]{:S(2)}) async-start(bf16[128,8,512]{2,0,1:T(8,128)(2,1)} %bitcast.193), calls=%async_computation | async-start | bytes 2097152 | tf_op jit(solution)/shard_map/all_to_all | solution.py:54
  81.8 2.0 copy.23
  86.3 2.3 constant_dynamic-update-slice_fusion.1
  88.6 2.3 constant_dynamic-update-slice_fusion
  90.9 1.5 collective-permute-start
  92.4 1.4 collective-permute-start.1
  93.8 9.1 %all-to-all-done = bf16[128,8,512]{2,0,1:T(8,128)(2,1)S(1)} async-done(((bf16[128,8,512]{2,0,1:T(8,128)(2,1)}), bf16[128,8,512]{2,0,1:T(8,128)(2,1)S(1)}, u32[]{:S(2)}, u32[]{:S(2)}) %all-to-all-start) | async-done | bytes 1048608 | tf_op jit(solution)/shard_map/all_to_all | solution.py:54
  104.0 1.6 copy.26
  105.6 1.5 broadcast.129.clone.1
  107.1 11.4 %while.40 = (s32[]{:T(128)}, f32[2,512,4]{1,2,0:T(4,128)S(1)}, f32[2,512,4]{1,2,0:T(4,128)S(1)}, f32[2,512,4,128]{3,1,2,0:T(8,128)}, bf16[2,512,4,128]{3,1,2,0:T...) while((s32[]{:T(128)}, f32[2,512,4]{1,2,0:T(4,128)S(1)}, ...), condition=%wide.region_3.4_spmd, body=%wide.region_0.3_spmd.sunk | while | flops 1090787328 | bytes 45703320 | solution.py:40
  107.1 1.3 bitcast_reduce_fusion.6
  108.7 2.2 fusion.118
  110.9 1.9 fusion.116
  112.9 1.3 bitcast_reduce_fusion.6
  114.5 2.2 fusion.118
  116.7 1.9 fusion.116
  118.6 22.0 %collective-permute-done = bf16[2,1024,4,128]{1,3,2,0:T(8,128)(2,1)} collective-permute-done((bf16[2,1024,4,128]{1,3,2,0:T(8,128)(2,1)}, bf16[2,1024,4,128]{1,3,2,0:T(8,128)(2,1)}, u32[]{:S(2)}, u32[]{:S(2)}) %collective-permute-start) | collective-permute-done | bytes 2097184 | tf_op jit(solution)/shard_map/ppermute | solution.py:13
  140.6 2.8 slice_bitcast_fusion.2
  143.4 1.6 copy.30
  145.0 1.3 copy.31
  146.3 1.5 broadcast.129.clone
  147.8 13.7 %while.41 = (s32[]{:T(128)}, f32[2,512,4]{1,2,0:T(4,128)S(1)}, f32[2,512,4]{1,2,0:T(4,128)S(1)}, f32[2,512,4,128]{3,1,2,0:T(8,128)}, f32[2,512,4]{1,2,0:T(4,128)...) while((s32[]{:T(128)}, f32[2,512,4]{1,2,0:T(4,128)S(1)}, ...), condition=%wide.region_8.9_spmd, body=%wide.region_5.8_spmd.sunk | while | flops 1095249920 | bytes 59367672 | solution.py:40
  147.8 1.3 bitcast_reduce_fusion.7
  150.3 2.2 fusion.125
  152.5 2.1 fusion.123
  154.7 1.3 bitcast_reduce_fusion.7
  157.2 2.2 fusion.125
  159.4 2.1 fusion.123
  161.5 23.4 %collective-permute-done.1 = bf16[2,1024,4,128]{1,3,2,0:T(8,128)(2,1)} collective-permute-done((bf16[2,1024,4,128]{1,3,2,0:T(8,128)(2,1)}, bf16[2,1024,4,128]{1,3,2,0:T(8,128)(2,1)}, u32[]{:S(2)}, u32[]{:S(2)}) %collective-permute-start.1) | collective-permute-done | bytes 2097184 | tf_op jit(solution)/shard_map/ppermute | solution.py:13
  185.0 2.8 slice_bitcast_fusion
  187.7 1.6 copy.33
  190.7 1.5 broadcast.129
  192.2 13.7 %while.42 = (s32[]{:T(128)}, f32[2,512,4]{1,2,0:T(4,128)S(1)}, f32[2,512,4,128]{3,1,2,0:T(8,128)}, f32[2,512,4]{1,2,0:T(4,128)S(1)}, f32[2,512,4]{1,2,0:T(4,128)...) while((s32[]{:T(128)}, f32[2,512,4]{1,2,0:T(4,128)S(1)}, ...), condition=%wide.region_13.14_spmd, body=%wide.region_10.13_spmd.sunk | while | flops 1095249920 | bytes 59359472 | solution.py:40
  192.2 1.3 bitcast_reduce_fusion.8
  194.7 2.2 fusion.132
  196.9 2.1 fusion.130
  199.1 1.3 bitcast_reduce_fusion.8
  201.5 2.2 fusion.132
  203.8 2.1 fusion.130
  205.9 2.2 divide_convert_fusion
  210.1 82.4 %all-gather.2.cloned.1.call-done = bf16[1024,4096]{1,0:T(8,128)(2,1)} async-done(((bf16[1024,512]{1,0:T(8,128)(2,1)}), bf16[1024,4096]{1,0:T(8,128)(2,1)}) %all-gather.2.cloned.1.call-update) | async-done | bytes 8388624 | tf_op jit(solution)/shard_map/all_gather | solution.py:90
  292.4 11.8 %convolution_convert_fusion = bf16[1024,768]{1,0:T(8,128)(2,1)} fusion(bf16[1024,4096]{1,0:T(8,128)(2,1)} %all-gather.2.cloned.1.call-done, bf16[4096,768]{1,0:T(8,128)(2,1)} %param.14), kind=kOutput, calls=%fused_computation.78 | convolution fusion | flops 6443237376 | bytes 16252928 | tf_op jit(solution)/shard_map/dot_general | solution.py:89
  (82 shorter events, 18.1 us)
Async XLA Ops:
  6.5 38.8 %copy-start.10 = (bf16[128,4096]{1,0:T(8,128)(2,1)S(1)}, bf16[128,4096]{1,0:T(8,128)(2,1)}, u32[]{:S(2)}) copy-start(bf16[128,4096]{1,0:T(8,128)(2,1)} %param.11) | copy-start | bytes 3145732
  6.5 70.0 %copy-start.13 = (s32[4,4]{1,0:T(4,128)S(1)}, s32[4,4]{1,0:T(4,128)}, u32[]{:S(2)}) copy-start(s32[4,4]{1,0:T(4,128)} %param.15) | copy-start | bytes 196
  8.9 32.9 %all-to-all-start.1 = ((bf16[128,8,512]{0,2,1:T(8,128)(2,1)}), bf16[128,8,512]{0,2,1:T(8,128)(2,1)S(1)}, u32[]{:S(2)}, u32[]{:S(2)}) async-start(bf16[128,8,512]{0,2,1:T(8,128)(2,1)} %bitcast.23), calls=%async_computation.1 | async-start | bytes 2097152 | tf_op jit(solution)/shard_map/all_to_all | solution.py:55
  41.8 30.1 %all-to-all-start.2 = ((bf16[128,8,512]{0,2,1:T(8,128)(2,1)}), bf16[128,8,512]{0,2,1:T(8,128)(2,1)S(1)}, u32[]{:S(2)}, u32[]{:S(2)}) async-start(bf16[128,8,512]{0,2,1:T(8,128)(2,1)} %bitcast.25), calls=%async_computation.2 | async-start | bytes 2097152 | tf_op jit(solution)/shard_map/all_to_all | solution.py:56
  71.9 1.0 copy-start.2
  72.8 30.1 %all-to-all-start = ((bf16[128,8,512]{2,0,1:T(8,128)(2,1)}), bf16[128,8,512]{2,0,1:T(8,128)(2,1)S(1)}, u32[]{:S(2)}, u32[]{:S(2)}) async-start(bf16[128,8,512]{2,0,1:T(8,128)(2,1)} %bitcast.193), calls=%async_computation | async-start | bytes 2097152 | tf_op jit(solution)/shard_map/all_to_all | solution.py:54
  76.4 216.0 %all-gather.2.cloned.1.call-start = ((), (), s32[]{:S(2)}) async-start(), calls=%async_computation.3 | async-start | bytes 9437184 | tf_op jit(solution)/shard_map/all_gather | solution.py:90
  81.8 21.6 %copy-start.3 = (bf16[1024,4,128]{0,2,1:T(8,128)(2,1)S(1)}, bf16[1024,4,128]{0,2,1:T(8,128)(2,1)}, u32[]{:S(2)}) copy-start(bf16[1024,4,128]{0,2,1:T(8,128)(2,1)} %squeeze.55) | copy-start | bytes 3145732
  90.9 49.7 %collective-permute-start = (bf16[2,1024,4,128]{1,3,2,0:T(8,128)(2,1)}, bf16[2,1024,4,128]{1,3,2,0:T(8,128)(2,1)}, u32[]{:S(2)}, u32[]{:S(2)}) collective-permute-start(bf16[2,1024,4,128]{1,3,2,0:T(8,128)(2,1)} %constant_dynamic-update-slice_fusion), channel_id=1, source_target_pairs={{0,8},{8,16},{16,24},{24,0},{1,9},{9,17},{17,25},{25,1},{2,10},{10... | collective-permute-start | bytes 6291464 | tf_op jit(solution)/shard_map/ppermute | solution.py:13
  92.4 92.6 %collective-permute-start.1 = (bf16[2,1024,4,128]{1,3,2,0:T(8,128)(2,1)}, bf16[2,1024,4,128]{1,3,2,0:T(8,128)(2,1)}, u32[]{:S(2)}, u32[]{:S(2)}) collective-permute-start(bf16[2,1024,4,128]{1,3,2,0:T(8,128)(2,1)} %constant_dynamic-update-slice_fusion), channel_id=1, source_target_pairs={{0,24},{8,0},{16,8},{24,16},{1,25},{9,1},{17,9},{25,17},{2,26},{10... | collective-permute-start | bytes 6291464 | tf_op jit(solution)/shard_map/ppermute | solution.py:13
  107.1 1.6 copy-start.4
  110.9 1.9 copy-start.5
  112.9 1.6 copy-start.4
  116.7 1.9 copy-start.5
  147.8 1.6 copy-start.6
  147.8 2.2 copy-start.7
  147.8 2.5 copy-start.11
  152.5 2.1 copy-start.8
  154.7 1.6 copy-start.6
  154.7 2.2 copy-start.7
  154.7 2.5 copy-start.11
  159.4 2.1 copy-start.8
  192.2 1.6 copy-start
  192.2 2.2 copy-start.9
  192.2 2.5 copy-start.12
  196.9 2.1 copy-start.1
  199.0 1.6 copy-start
  199.0 2.2 copy-start.9
  199.1 2.5 copy-start.12
  203.8 2.1 copy-start.1
Sparse Core Ops, SparseCore 0:
  210.2 82.1 all-gather.1
where the time goes:
time: 312 us; the launch traced here: 311 us
  waiting for transfers between devices  187 us (60%)
  local copies, waits for them, and re-layouts  44.5 us (14%)
  matrix products  33.1 us (11%)
  starting transfers between devices  16.4 us (5%)
  other arithmetic  15.2 us (5%)
  between operations  14.9 us (5%)
    all_gather x1, waiting for transfers between devices, body(): lax.all_gather(attended, 'space', axis=1, tiled=True)  82.4 us
    ppermute x2, waiting for transfers between devices, passed_along(): lax.ppermute(x, axis, [(i, (i + by) % devices) for i in range(devices)])  45.5 us
    all_to_all x1, waiting for transfers between devices, body(): lax.all_to_all(value_vectors, 'space', split_axis=1, concat_axis=0, tiled...  25.4 us
    all_to_all x1, waiting for transfers between devices, body(): lax.all_to_all(key_vectors, 'space', split_axis=1, concat_axis=0, tiled=T...  24.3 us
    dot_general x6, matrix products, one_block(): jnp.einsum('qhk,khd->qhd', exp_terms.astype(jnp.bfloat16), values_here, p...  13.3 us
    reduce_sum x6, other arithmetic, one_block(): new_total = old_total * rescale + jnp.sum(exp_terms, axis=2)  12 us
    dot_general x1, matrix products, body(): jnp.dot(lax.all_gather(attended, 'space', axis=1, tiled=True), out_weight...  11.8 us
    all_to_all x1, waiting for transfers between devices, body(): lax.all_to_all(queries, 'space', split_axis=1, concat_axis=0, tiled=True)  9.06 us
  transfers between devices with their start and end apart: 6, of which 6 were waited for; matrix products, arithmetic and copies ran while one was open for 16% of the time, Pallas kernels for 0%

commit v1 on v0

v1 whole, which is shorter than its diff:
```python
import functools
import math

import jax
import jax.numpy as jnp
from jax import lax
from jax.experimental import pallas as pl
from jax.experimental.pallas import tpu as pltpu
from jax.sharding import PartitionSpec as P

HD = 128
MESH = pl.DeviceIdType.MESH


def kernel(
    frames, places, heads,
    q_hbm, k_hbm, v_hbm, w_hbm, mask_ref, out_ref,
    qb, kvb, kvx, kvy, gat, wv, acc,
    a_send, a_recv, x_send, x_recv, y_send, y_recv,
    g_send, g_recv, p_recv, w_sem,
):
    f = lax.axis_index("tm")
    s = lax.axis_index("space")
    tok = q_hbm.shape[0]
    rows = tok * places
    chips = places // 2
    z = lax.div(s, 2)
    core = lax.rem(s, 2)
    odd = lax.rem(f, 2)
    partner = f + 1 - 2 * odd
    onward = lax.rem(f + 2 - 4 * odd + frames, frames)
    behind = lax.rem(f - 2 + 4 * odd + frames, frames)
    far = lax.rem(f - 1 + 2 * odd + frames, frames)
    mate = 2 * z + 1 - core

    barrier = pltpu.get_barrier_semaphore()

    def greet(j, carry):
        pl.semaphore_signal(
            barrier, inc=1, device_id=(f, lax.rem(s + j, places)), device_id_type=MESH
        )
        return carry

    lax.fori_loop(1, places, greet, 0)
    for other in (partner, onward, behind):
        pl.semaphore_signal(barrier, inc=1, device_id=(other, s), device_id_type=MESH)
    pl.semaphore_wait(barrier, places - 1 + 3)

    def remote(src, dst, send, recv, tm_to, space_to):
        return pltpu.make_async_remote_copy(
            src_ref=src, dst_ref=dst, send_sem=send, recv_sem=recv,
            device_id=(tm_to, space_to), device_id_type=MESH,
        )

    def landing(t, h):
        return qb.at[h] if t == 2 else kvb.at[t, h]

    sources = (k_hbm, v_hbm, q_hbm)

    def send_head(h):
        for t in range(3):
            mine = landing(t, h).at[pl.ds(pl.multiple_of(s * tok, tok), tok), :]

            def one(j, carry):
                to = lax.rem(s + j, places)
                cols = pl.ds(pl.multiple_of((to * heads + h) * HD, HD), HD)
                remote(
                    sources[t].at[:, cols], mine, a_send.at[h, t], a_recv.at[h, t], f, to
                ).start()
                return carry

            lax.fori_loop(1, places, one, 0)
            cols = pl.ds(pl.multiple_of((s * heads + h) * HD, HD), HD)
            pltpu.make_async_copy(sources[t].at[:, cols], mine, a_recv.at[h, t]).start()

    def whole_wait(ref, sem):
        pltpu.make_async_copy(ref, ref, sem).wait()

    def x_copy(h, t):
        return remote(
            kvb.at[t, h], kvx.at[t, h], x_send.at[h, t], x_recv.at[h, t], partner, s
        )

    def y_copy(h, t):
        return remote(
            kvx.at[t, h], kvy.at[t, h], y_send.at[h, t], y_recv.at[h, t], onward, s
        )

    def columns(place):
        return pl.ds(pl.multiple_of(place * HD, HD), HD)

    def g_copy(g, place, slot, recv, to):
        part = gat.at[g, :, columns(place)]
        return remote(part, part, g_send.at[g, slot], recv, f, to)

    def own_copies(g):
        return [
            (z < chips - 1, g_copy(g, s, 0, g_recv.at[g, 0, 0], s + 2)),
            (z > 0, g_copy(g, s, 1, g_recv.at[g, 1, 0], s - 2)),
            (None, g_copy(g, s, 2, p_recv.at[g, z], mate)),
        ]

    def relay_copies(g, k):
        low, high = s - 2 * k, s + 2 * k
        base = 3 + 4 * (k - 1)
        copies = []
        if k < chips - 1:
            copies.append(((z >= k) & (z < chips - 1),
                           lambda: g_copy(g, low, base, g_recv.at[g, 0, k], s + 2)))
        copies.append((z >= k, lambda: g_copy(g, low, base + 1, p_recv.at[g, z - k], mate)))
        if k < chips - 1:
            copies.append(((z + k <= chips - 1) & (z > 0),
                           lambda: g_copy(g, high, base + 2, g_recv.at[g, 1, k], s - 2)))
        copies.append((z + k <= chips - 1,
                       lambda: g_copy(g, high, base + 3, p_recv.at[g, z + k], mate)))
        return copies

    def start_own(g):
        for cond, copy in own_copies(g):
            if cond is None:
                copy.start()
            else:
                pl.when(cond)(copy.start)

    def relay(g, k):
        @pl.when(z >= k)
        def _():
            g_copy(g, s - 2 * k, 0, g_recv.at[g, 0, k - 1], mate).wait_recv()

        @pl.when(z + k <= chips - 1)
        def _():
            g_copy(g, s + 2 * k, 0, g_recv.at[g, 1, k - 1], mate).wait_recv()

        for cond, make in relay_copies(g, k):
            @pl.when(cond)
            def _():
                make().start()

    near_pen = jnp.where(mask_ref[f, partner] == 1, 0.0, jnp.inf).astype(jnp.float32)
    far_pen = jnp.where(mask_ref[f, far] == 1, 0.0, jnp.inf).astype(jnp.float32)
    factor = math.log2(math.e) / math.sqrt(HD)
    q_tile = min(256, rows)
    tiles = rows // q_tile

    def attend(h, first, last):
        def tile(i, carry):
            at = pl.ds(pl.multiple_of(i * q_tile, q_tile), q_tile)
            q = qb[h, at, :]
            places_kv = ((kvb, None), (kvx, near_pen), (kvy, far_pen))
            scores = []
            top = None
            for ref, pen in places_kv:
                sc = lax.dot_general(
                    q, ref[0, h], (((1,), (1,)), ((), ())),
                    preferred_element_type=jnp.float32,
                )
                scores.append(sc)
                best = jnp.max(sc, axis=1, keepdims=True)
                best = best if pen is None else best - pen
                top = best if top is None else jnp.maximum(top, best)
            total = None
            mixed = None
            for sc, (ref, pen) in zip(scores, places_kv):
                level = top if pen is None else top + pen
                e = jnp.exp2((sc - level) * factor)
                part = jnp.sum(e, axis=1, keepdims=True)
                prod = jnp.dot(
                    e.astype(jnp.bfloat16), ref[1, h], preferred_element_type=jnp.float32
                )
                total = part if total is None else total + part
                mixed = prod if mixed is None else mixed + prod
            gat[h, at, columns(s)] = (mixed / total).astype(jnp.bfloat16)
            return carry

        lax.fori_loop(first, last, tile, 0)

    p_tile = min(256, rows)

    def project(g):
        for o in range(chips):
            g_copy(g, 2 * o + 1 - core, 0, p_recv.at[g, o], mate).wait_recv()
        whole_wait(wv.at[g], w_sem.at[g])

        def tile(i, carry):
            at = pl.ds(pl.multiple_of(i * p_tile, p_tile), p_tile)
            prod = jnp.dot(gat[g, at, :], wv[g], preferred_element_type=jnp.float32)
            if g > 0:
                prod = prod + acc[at, :]
            if g == heads - 1:
                out_ref[at, :] = prod.astype(out_ref.dtype)
            else:
                acc[at, :] = prod
            return carry

        lax.fori_loop(0, rows // p_tile, tile, 0)

    events = [(g, k) for g in range(heads) for k in range(1, chips)]
    done = [0]

    def relay_some(count, limit_group):
        while count > 0 and done[0] < len(events) and events[done[0]][0] <= limit_group:
            g, k = events[done[0]]
            relay(g, k)
            done[0] += 1
            count -= 1
            if k == chips - 1 and limit_group >= heads - 1:
                project(g)

    for h in range(min(2, heads)):
        send_head(h)
    for h in range(heads):
        def load(i, carry):
            pltpu.make_async_copy(
                w_hbm.at[pl.ds(pl.multiple_of((i * heads + h) * HD, HD), HD), :],
                wv.at[h, pl.ds(pl.multiple_of(i * HD, HD), HD), :],
                w_sem.at[h],
            ).start()
            return carry

        lax.fori_loop(0, places, load, 0)

    for step in range(heads + 1):
        if step < heads:
            for t in range(2):
                whole_wait(kvb.at[t, step], a_recv.at[step, t])
                x_copy(step, t).start()
            if step + 2 < heads:
                send_head(step + 2)
            for t in range(2):
                x_copy(step, t).wait_recv()
                y_copy(step, t).start()
        h = step - 1
        if h < 0:
            continue
        if h >= 2:
            relay_some(1, h - 2)
        whole_wait(qb.at[h], a_recv.at[h, 2])
        for t in range(2):
            y_copy(h, t).wait_recv()
        if h == heads - 1:
            attend(h, 0, tiles // 2)
            relay_some(2, h - 1)
            attend(h, tiles // 2, tiles)
        else:
            attend(h, 0, tiles)
        start_own(h)
    for g in range(done[0] // (chips - 1)):
        project(g)
    relay_some(len(events), heads - 1)

    for h in range(heads):
        for t in range(3):
            part = landing(t, h).at[pl.ds(0, (places - 1) * tok), :]
            whole_wait(part, a_send.at[h, t])
        for t in range(2):
            x_copy(h, t).wait_send()
            y_copy(h, t).wait_send()
        for cond, copy in own_copies(h):
            if cond is None:
                copy.wait_send()
            else:
                pl.when(cond)(copy.wait_send)
        for k in range(1, chips):
            for cond, make in relay_copies(h, k):
                @pl.when(cond)
                def _():
                    make().wait_send()


def solution(mesh):
    frames = mesh.shape["tm"]
    places = mesh.shape["space"]

    def body(queries, key_vectors, value_vectors, out_weight, frame_mask):
        tok, width = queries.shape
        heads = width // HD // places
        rows = tok * places
        chips = places // 2
        cols = out_weight.shape[1]
        bf16 = jnp.bfloat16
        anyspace = pl.BlockSpec(memory_space=pl.ANY)
        dma = pltpu.SemaphoreType.DMA
        return pl.pallas_call(
            functools.partial(kernel, frames, places, heads),
            out_shape=jax.ShapeDtypeStruct((rows, cols), bf16),
            in_specs=[anyspace] * 4 + [pl.BlockSpec(memory_space=pltpu.SMEM)],
            out_specs=pl.BlockSpec(memory_space=pltpu.VMEM),
            scratch_shapes=[
                pltpu.VMEM((heads, rows, HD), bf16),
                pltpu.VMEM((2, heads, rows, HD), bf16),
                pltpu.VMEM((2, heads, rows, HD), bf16),
                pltpu.VMEM((2, heads, rows, HD), bf16),
                pltpu.VMEM((heads, rows, places * HD), bf16),
                pltpu.VMEM((heads, places * HD, cols), bf16),
                pltpu.VMEM((rows, cols), jnp.float32),
                dma((heads, 3)), dma((heads, 3)),
                dma((heads, 2)), dma((heads, 2)),
                dma((heads, 2)), dma((heads, 2)),
                dma((heads, 3 + 4 * (chips - 1))),
                dma((heads, 2, chips - 1)),
                dma((heads, chips)),
                dma((heads,)),
            ],
            compiler_params=pltpu.CompilerParams(
                collective_id=0, has_side_effects=True,
                vmem_limit_bytes=60 * 1024 * 1024,
            ),
        )(queries, key_vectors, value_vectors, out_weight, frame_mask)

    in_specs = (
        P(("tm", "space"), None),
        P(("tm", "space"), None),
        P(("tm", "space"), None),
        P(None, "space"),
        P(),
    )
    return jax.shard_map(
        body, mesh=mesh, in_specs=in_specs, out_specs=P("tm", "space"), check_vma=False
    )
```

time: 312 us -> 160 us (0.51)
  waiting for transfers between devices: 187 us -> 0 us
  Pallas kernels: 0 us -> 156 us
  local copies, waits for them, and re-layouts: 44.5 us -> 2.65 us
  matrix products: 33.1 us -> 0 us
  starting transfers between devices: 16.4 us -> 0 us
  other arithmetic: 15.2 us -> 0 us
  between operations: 14.9 us -> 0.01 us
    pallas_call x0 -> x1, Pallas kernels: none -> 156 us  [body(): pl.pallas_call(functools.partial(kernel, frames, places, heads), out_shap...]
    all_gather x1 -> x0, waiting for transfers between devices: 82.4 us -> none  [body(): lax.all_gather(attended, 'space', axis=1, tiled=True)]
    all_to_all x3 -> x0, waiting for transfers between devices: 58.8 us -> none  [the longest x1 25.4 us: body(): lax.all_to_all(value_vectors, 'space', split_axis=1, concat_axis=0, tiled...]
    ppermute x2 -> x0, waiting for transfers between devices: 45.5 us -> none  [passed_along(): lax.ppermute(x, axis, [(i, (i + by) % devices) for i in range(devices)])]
    dot_general x13 -> x0, matrix products: 33.1 us -> none  [the longest x6 13.3 us: one_block(): jnp.einsum('qhk,khd->qhd', exp_terms.astype(jnp.bfloat16), values_here, p...]
    all_to_all x3 -> x0, starting transfers between devices: 13.5 us -> none  [the longest x1 6.35 us: body(): lax.all_to_all(key_vectors, 'space', split_axis=1, concat_axis=0, tiled=T...]
    while x47 -> x0, local copies, waits for them, and re-layouts: 13.1 us -> none  [the longest x7 8.25 us: block_update(): return lax.map(one_block, (query_blocks, run_max, run_total, run_sum))]
    reduce_sum x7 -> x0, other arithmetic: 12.8 us -> none  [the longest x6 12 us: one_block(): new_total = old_total * rescale + jnp.sum(exp_terms, axis=2)]
  transfers between devices with their start and end apart: 6 -> 0, of which waited for: 6 -> 0; matrix products, arithmetic and copies ran while one was open for 16% -> 0% of each run, Pallas kernels for 0% -> 0%
where the time goes in v1:
time: 160 us; the launch traced here: 159 us
  Pallas kernels  156 us (98%)
  local copies, waits for them, and re-layouts  2.65 us (2%)
    pallas_call x1, Pallas kernels, body(): pl.pallas_call(functools.partial(kernel, frames, places, heads), out_shap...  156 us

profile of v1, /device:TPU:0, one launch (start us, length us, event | category | flops | bytes accessed | tf_op | source)
XLA Modules:
  0.0 158.8 jit_solution(12395253597377946697)
XLA Ops:
  0.0 156.1 %shard_map.55 = bf16[1024,768]{1,0:T(8,128)(2,1)} custom-call(bf16[128,4096]{1,0:T(8,128)(2,1)} %q_hbm.1, bf16[128,4096]{1,0:T(8,128)(2,1)} %k_hbm.1, bf16[128,4096]{1,0:T(8,128)(2,1)} %v_hbm.1, bf16[4096,768]{1,0:T(8,128)(2,1)} %w_hbm.1, s32[4,4]{1,0:T(4,128)} %mask_ref.1), custom_call_target="tpu_custom_call" | custom-call | tf_op jit(solution)/shard_map/pallas_call | solution.py:283
  156.1 2.7 %copy.7 = bf16[1024,768]{1,0:T(8,128)(2,1)} copy(bf16[1024,768]{1,0:T(8,128)(2,1)} %shard_map.55) | data formatting | bytes 3145728

commit v2 on v1

--- a/solution.py
+++ b/solution.py
@@ -23,6 +23,7 @@
     s = lax.axis_index("space")
     tok = q_hbm.shape[0]
     rows = tok * places
+    half = rows // 2
     chips = places // 2
     z = lax.div(s, 2)
     core = lax.rem(s, 2)
@@ -90,7 +91,7 @@
         return pl.ds(pl.multiple_of(place * HD, HD), HD)
 
     def g_copy(g, place, slot, recv, to):
-        part = gat.at[g, :, columns(place)]
+        part = gat.at[g // 2, pl.ds(g % 2 * half, half), columns(place)]
         return remote(part, part, g_send.at[g, slot], recv, f, to)
 
     def own_copies(g):
@@ -139,7 +140,7 @@
     near_pen = jnp.where(mask_ref[f, partner] == 1, 0.0, jnp.inf).astype(jnp.float32)
     far_pen = jnp.where(mask_ref[f, far] == 1, 0.0, jnp.inf).astype(jnp.float32)
     factor = math.log2(math.e) / math.sqrt(HD)
-    q_tile = min(256, rows)
+    q_tile = min(256, half)
     tiles = rows // q_tile
 
     def attend(h, first, last):
@@ -174,15 +175,17 @@
 
         lax.fori_loop(first, last, tile, 0)
 
-    p_tile = min(256, rows)
-
-    def project(g):
+    p_tile = min(256, half)
+
+    def project(c):
+        g = c // 2
         for o in range(chips):
-            g_copy(g, 2 * o + 1 - core, 0, p_recv.at[g, o], mate).wait_recv()
-        whole_wait(wv.at[g], w_sem.at[g])
+            g_copy(c, 2 * o + 1 - core, 0, p_recv.at[c, o], mate).wait_recv()
+        if c % 2 == 0:
+            whole_wait(wv.at[g], w_sem.at[g])
 
         def tile(i, carry):
-            at = pl.ds(pl.multiple_of(i * p_tile, p_tile), p_tile)
+            at = pl.ds(pl.multiple_of(c % 2 * half + i * p_tile, p_tile), p_tile)
             prod = jnp.dot(gat[g, at, :], wv[g], preferred_element_type=jnp.float32)
             if g > 0:
                 prod = prod + acc[at, :]
@@ -192,19 +195,29 @@
                 acc[at, :] = prod
             return carry
 
-        lax.fori_loop(0, rows // p_tile, tile, 0)
-
-    events = [(g, k) for g in range(heads) for k in range(1, chips)]
+        lax.fori_loop(0, half // p_tile, tile, 0)
+
+    chunks = 2 * heads
+    events = sorted(
+        ((c // 2 + k, c, k) for c in range(chunks) for k in range(1, chips))
+    )
     done = [0]
-
-    def relay_some(count, limit_group):
-        while count > 0 and done[0] < len(events) and events[done[0]][0] <= limit_group:
-            g, k = events[done[0]]
-            relay(g, k)
+    sent = set()
+    ready = []
+
+    def send_own(c):
+        start_own(c)
+        sent.add(c)
+
+    def relay_upto(rank):
+        while done[0] < len(events):
+            key, c, k = events[done[0]]
+            if key > rank or c not in sent:
+                return
+            relay(c, k)
             done[0] += 1
-            count -= 1
-            if k == chips - 1 and limit_group >= heads - 1:
-                project(g)
+            if k == chips - 1:
+                ready.append(c)
 
     for h in range(min(2, heads)):
         send_head(h)
@@ -220,33 +233,41 @@
         lax.fori_loop(0, places, load, 0)
 
     for step in range(heads + 1):
+        h = step - 1
         if step < heads:
             for t in range(2):
                 whole_wait(kvb.at[t, step], a_recv.at[step, t])
                 x_copy(step, t).start()
             if step + 2 < heads:
                 send_head(step + 2)
+        if h >= 0:
+            whole_wait(qb.at[h], a_recv.at[h, 2])
+            for t in range(2):
+                y_copy(h, t).wait_recv()
+            attend(h, 0, tiles // 2)
+            send_own(2 * h)
+        if step < heads:
             for t in range(2):
                 x_copy(step, t).wait_recv()
                 y_copy(step, t).start()
-        h = step - 1
-        if h < 0:
-            continue
-        if h >= 2:
-            relay_some(1, h - 2)
-        whole_wait(qb.at[h], a_recv.at[h, 2])
-        for t in range(2):
-            y_copy(h, t).wait_recv()
-        if h == heads - 1:
-            attend(h, 0, tiles // 2)
-            relay_some(2, h - 1)
+        if h >= heads - 2:
+            relay_upto(1 if h == heads - 2 else 3)
+        if h >= 0:
             attend(h, tiles // 2, tiles)
+            send_own(2 * h + 1)
+        if h == heads - 2:
+            relay_upto(2)
+    while done[0] < len(events):
+        key = events[done[0]][0]
+        if key == events[-1][0]:
+            key, c, k = events[done[0]]
+            relay(c, k)
+            done[0] += 1
+            ready.append(c)
         else:
-            attend(h, 0, tiles)
-        start_own(h)
-    for g in range(done[0] // (chips - 1)):
-        project(g)
-    relay_some(len(events), heads - 1)
+            relay_upto(key)
+        while ready:
+            project(ready.pop(0))
 
     for h in range(heads):
         for t in range(3):
@@ -255,13 +276,14 @@
         for t in range(2):
             x_copy(h, t).wait_send()
             y_copy(h, t).wait_send()
-        for cond, copy in own_copies(h):
+    for c in range(chunks):
+        for cond, copy in own_copies(c):
             if cond is None:
                 copy.wait_send()
             else:
                 pl.when(cond)(copy.wait_send)
         for k in range(1, chips):
-            for cond, make in relay_copies(h, k):
+            for cond, make in relay_copies(c, k):
                 @pl.when(cond)
                 def _():
                     make().wait_send()
@@ -296,9 +318,9 @@
                 dma((heads, 3)), dma((heads, 3)),
                 dma((heads, 2)), dma((heads, 2)),
                 dma((heads, 2)), dma((heads, 2)),
-                dma((heads, 3 + 4 * (chips - 1))),
-                dma((heads, 2, chips - 1)),
-                dma((heads, chips)),
+                dma((2 * heads, 3 + 4 * (chips - 1))),
+                dma((2 * heads, 2, chips - 1)),
+                dma((2 * heads, chips)),
                 dma((heads,)),
             ],
             compiler_params=pltpu.CompilerParams(

time: 160 us -> 152 us (0.950)
  Pallas kernels: 156 us -> 149 us
    pallas_call x1, Pallas kernels: 156 us -> 149 us  [body(): pl.pallas_call(functools.partial(kernel, frames, places, heads), out_shap...]
where the time goes in v2:
time: 152 us
  Pallas kernels  149 us (98%)
  local copies, waits for them, and re-layouts  2.65 us (2%)
    pallas_call x1, Pallas kernels, body(): pl.pallas_call(functools.partial(kernel, frames, places, heads), out_shap...  149 us

profile of v2, /device:TPU:0, one launch (start us, length us, event | category | flops | bytes accessed | tf_op | source)
XLA Modules:
  0.0 151.6 jit_solution(14826500163046942545)
XLA Ops:
  0.0 148.9 %shard_map.55 = bf16[1024,768]{1,0:T(8,128)(2,1)} custom-call(bf16[128,4096]{1,0:T(8,128)(2,1)} %q_hbm.1, bf16[128,4096]{1,0:T(8,128)(2,1)} %k_hbm.1, bf16[128,4096]{1,0:T(8,128)(2,1)} %v_hbm.1, bf16[4096,768]{1,0:T(8,128)(2,1)} %w_hbm.1, s32[4,4]{1,0:T(4,128)} %mask_ref.1), custom_call_target="tpu_custom_call" | custom-call | tf_op jit(solution)/shard_map/pallas_call | solution.py:305
  148.9 2.7 %copy.7 = bf16[1024,768]{1,0:T(8,128)(2,1)} copy(bf16[1024,768]{1,0:T(8,128)(2,1)} %shard_map.55) | data formatting | bytes 3145728
